TPU v7x, 512 devices: a 8x2x16 block of a 8x8x16 slice. The times are simulated.
512 devices in a mesh: groups: 2 (over y), seq: 16 (over z), head: 8 (over x), rep: 2 (over core).
Axes of the slice: x: 8, y: 2, z: 16, core: 2. Of those that a mesh axis runs over, the one named last changes fastest.
The devices are a block of a 8x8x16 slice.
Arguments:
- queries: bfloat16 [512, 64, 128], P(('groups', 'seq', 'rep'), 'head'), parts along dimension 0, may hold values from -256 to 256
- page_owner: int32 [512, 128], P(('groups', 'seq', 'rep')), parts along dimension 0, may hold values from -1 to 15, as said below
- page_slot: int32 [512, 128], P(('groups', 'seq', 'rep')), parts along dimension 0, may hold values from -1 to 63, as said below
- lengths: int32 [512], P(('groups', 'seq', 'rep')), parts along dimension 0, may hold values from 1 to 16384, as said below
- keys: bfloat16 [4096, 8, 128, 128], P(('groups', 'seq', 'rep'), 'head'), parts along dimension 0, may hold values from -24 to 24
- values: bfloat16 [4096, 8, 128, 128], P(('groups', 'seq', 'rep'), 'head'), parts along dimension 0, may hold values from -6 to 6
Outputs:
- attended: bfloat16 [512, 64, 128], P(('groups', 'seq', 'rep'), 'head'), parts along dimension 0
There are 2 independent parts, one for each index of `groups`. A program takes and returns all parts, laid end to end along the dimension named above; each array names one. Nothing has to cross between parts.
Inputs may be any that keep to these rules, and one draw needn't show every extreme that they name: `page_owner`: for j below ceil(lengths[r] / 128) the seq index of the device, among those of r's half (r // 8) % 2, whose pool holds page j of r; -1 for later j. `page_slot`: the page's slot in that pool, -1 where page_owner is -1. No slot of a pool holds two pages; in each half, some device's pool has all 64 slots in use. `lengths`: in each half some request has the most.
All inputs are finite; a program needn't handle non-finite values.
Results may differ from a plain program's by a relative error of at most 0.0041.
Values may be sent and summed in bfloat16 or wider, within the bound.
No kernel may reach another device: no remote copies, remote signals or barrier semaphores. Data moves between devices by JAX's collectives and lax.ppermute only.
A program may use at most 64 MiB of HBM per device.

v0:
```python
import math

import jax
import jax.numpy as jnp
from jax import lax
from jax.sharding import PartitionSpec as P

masked_score = -1e30


def sent_to_all(x, axis):
    copies = jnp.broadcast_to(x, (lax.axis_size(axis), *x.shape))
    return lax.all_to_all(copies, axis, split_axis=0, concat_axis=0, tiled=True)


def laid_out(parts, dim):
    dims = list(parts.shape[1:])
    dims[dim] *= parts.shape[0]
    return jnp.moveaxis(parts, 0, dim).reshape(dims)


def collect(x, axis, dim):
    parts = sent_to_all(x, axis)
    return laid_out(parts, dim)


def sent_together(arrays, axis, split_dim, concat_dim, along):
    columns = [a.reshape(*a.shape[:along], -1) for a in arrays]
    both = jnp.concatenate(columns, axis=along)
    out, at, outs = (
        lax.all_to_all(both, axis, split_axis=split_dim, concat_axis=concat_dim, tiled=True),
        0,
        [],
    )
    for a, column in zip(arrays, columns):
        slab = out[..., at : at + column.shape[along]]
        outs.append(slab.reshape(*slab.shape[:along], *a.shape[along:]))
        at += column.shape[along]
    return tuple(outs)


def on_device(queries, page_owner, page_slot, lengths, keys, values):
    rows_own = queries.shape[0]
    head_count = queries.shape[1]
    head_width = queries.shape[2]
    pool_size = keys.shape[0]
    kv_heads = keys.shape[1]
    page_tokens = keys.shape[2]
    group_size = head_count // kv_heads
    most_pages = page_owner.shape[1]
    page_index = jnp.arange(most_pages, dtype=jnp.int32)
    own_live = jnp.clip(lengths[:, None] - page_index[None, :] * page_tokens, 0, page_tokens)
    packed = jnp.where(
        page_owner >= 0, (page_owner * pool_size + page_slot) * (page_tokens + 1) + own_live, -1
    )
    all_queries, all_packed = (collect(queries, "seq", 0), collect(packed, "seq", 0))
    present = all_packed >= 0
    safe_word = jnp.maximum(all_packed, 0)
    live_count = jnp.where(present, safe_word % (page_tokens + 1), 0).astype(jnp.int32)
    place_word = safe_word // (page_tokens + 1)
    all_owner = jnp.where(present, place_word // pool_size, -1).astype(jnp.int32)
    all_slot = jnp.where(present, place_word % pool_size, -1).astype(jnp.int32)
    rows_half = all_queries.shape[0]
    seq_index = lax.axis_index("seq")
    held_here = (all_owner == seq_index) & (live_count > 0)
    slot_index = jnp.arange(pool_size, dtype=jnp.int32)
    matches = held_here[None, :, :] & (all_slot[None, :, :] == slot_index[:, None, None])
    slot_owner = jnp.any(matches, axis=2)
    slot_tokens = jnp.sum(jnp.where(matches, live_count[None, :, :], 0), axis=(1, 2))
    picker = slot_owner.astype(jnp.bfloat16)
    flat_queries = all_queries.reshape(rows_half, head_count * head_width)
    slot_queries = jnp.dot(picker, flat_queries, preferred_element_type=jnp.float32)
    slot_queries = slot_queries.astype(jnp.bfloat16).reshape(
        pool_size, kv_heads, group_size, head_width
    )
    score_scale = 1.0 / math.sqrt(head_width)
    scores = (
        jnp.einsum("pkgd,pktd->pkgt", slot_queries, keys, preferred_element_type=jnp.float32)
        * score_scale
    )
    token_index = jnp.arange(page_tokens, dtype=jnp.int32)
    live_tokens = (token_index[None, :] < slot_tokens[:, None])[:, None, None, :]
    scores = jnp.where(live_tokens, scores, masked_score)
    page_max = jnp.max(scores, axis=3)
    weights = jnp.where(live_tokens, jnp.exp(scores - page_max[..., None]), 0.0)
    page_sum = jnp.sum(weights, axis=3)
    page_out = jnp.einsum(
        "pkgt,pktd->pkgd", weights.astype(jnp.bfloat16), values, preferred_element_type=jnp.float32
    )
    linked = slot_owner.T[:, :, None, None]
    request_max = jnp.max(jnp.where(linked, page_max[None], masked_score), axis=1)
    rescale = jnp.where(
        linked, jnp.exp(jnp.minimum(page_max[None] - request_max[:, None], 0.0)), 0.0
    )
    request_sum = jnp.sum(rescale * page_sum[None], axis=1)
    request_out = jnp.einsum("rpkg,pkgd->rkgd", rescale, page_out, precision=lax.Precision.HIGHEST)
    got_max, got_sum, got_out = sent_together(
        (request_max, request_sum, request_out), "seq", 0, 0, 3
    )
    sources = rows_half // rows_own
    got_max = got_max.reshape((sources, rows_own) + got_max.shape[1:])
    got_sum = got_sum.reshape((sources, rows_own) + got_sum.shape[1:])
    got_out = got_out.reshape((sources, rows_own) + got_out.shape[1:])
    overall = jnp.max(got_max, axis=0)
    source_scale = jnp.exp(got_max - overall[None])
    own_sum = jnp.sum(source_scale * got_sum, axis=0)
    own_out = jnp.sum(source_scale[..., None] * got_out, axis=0)
    attended = own_out / own_sum[..., None]
    return attended.astype(jnp.bfloat16).reshape(rows_own, head_count, head_width)


def solution(mesh):
    placed = (
        P(("groups", "seq", "rep"), "head", None),
        P(("groups", "seq", "rep"), None),
        P(("groups", "seq", "rep"), None),
        P(("groups", "seq", "rep")),
        P(("groups", "seq", "rep"), "head", None, None),
        P(("groups", "seq", "rep"), "head", None, None),
    )
    return jax.shard_map(
        on_device,
        mesh=mesh,
        in_specs=placed,
        out_specs=P(("groups", "seq", "rep"), "head", None),
        check_vma=False,
    )
```

profile of v0, /device:TPU:80, one launch (start us, length us, event | category | flops | bytes accessed | tf_op | source)
XLA Modules:
  0.0 148.8 jit_solution(8831032241151372216)
XLA Ops:
  0.0 0.9 add_select_fusion.4
  0.9 0.6 broadcast_in_dim.95
  1.6 43.7 %all-to-all-start = ((s32[16,8,128]{2,1,0:T(8,128)}), s32[16,8,128]{2,1,0:T(8,128)S(1)}, u32[]{:S(2)}, u32[]{:S(2)}) async-start(s32[16,8,128]{2,1,0:T(8,128)} %broadcast_in_dim.95), calls=%async_computation | async-start | bytes 131072 | tf_op jit(solution)/shard_map/all_to_all | solution.py:13
  45.3 12.7 %all-to-all-done = s32[16,8,128]{2,1,0:T(8,128)S(1)} async-done(((s32[16,8,128]{2,1,0:T(8,128)}), s32[16,8,128]{2,1,0:T(8,128)S(1)}, u32[]{:S(2)}, u32[]{:S(2)}) %all-to-all-start) | async-done | bytes 65568 | tf_op jit(solution)/shard_map/all_to_all | solution.py:13
  57.9 1.5 broadcast_in_dim.100
  59.4 4.0 %all-to-all-start.1 = ((bf16[16,8,8,128]{3,2,1,0:T(8,128)(2,1)}), bf16[16,8,8,128]{3,2,1,0:T(8,128)(2,1)S(1)}, u32[]{:S(2)}, u32[]{:S(2)}) async-start(bf16[16,8,8,128]{3,2,1,0:T(8,128)(2,1)} %broadcast_in_dim.100), calls=%async_computation.1 | async-start | bytes 524288 | tf_op jit(solution)/shard_map/all_to_all | solution.py:13
  63.4 0.1 compare_and_fusion
  63.5 0.1 fusion.32
  63.6 1.2 fusion.1
  64.8 1.3 select_reduce_fusion
  66.1 0.1 iota_compare_fusion.1
  66.1 14.3 %all-to-all-done.1 = bf16[16,8,8,128]{3,2,1,0:T(8,128)(2,1)S(1)} async-done(((bf16[16,8,8,128]{3,2,1,0:T(8,128)(2,1)}), bf16[16,8,8,128]{3,2,1,0:T(8,128)(2,1)S(1)}, u32[]{:S(2)}, u32[]{:S(2)}) %all-to-all-start.1) | async-done | bytes 262176 | tf_op jit(solution)/shard_map/all_to_all | solution.py:13
  80.4 0.2 fusion.12
  80.6 1.3 fusion.42
  81.9 0.2 fusion.21
  82.2 0.1 select_reduce_fusion.1
  82.3 2.3 %fusion.2 = f32[64,8,128]{2,1,0:T(8,128)S(1)} fusion(bf16[64,1,128,128]{3,2,1,0:T(8,128)(2,1)} %param.11, f32[64,8,128]{2,1,0:T(8,128)S(1)} %get-tuple-element.10, f32[64,8]{1,0:T(8,128)S(1)} %get-tuple-element.9, pred[64,128]{1,0:T(8,128)(4,1)S(1)} %iota_compare_fusion.1), kind=kOutput, calls=%fused_computation.4 | convolution fusion | flops 16973824 | bytes 2631680 | tf_op jit(solution)/shard_map/pkgt,pktd->pkgd/dot_general | solution.py:87
  84.6 0.2 multiply_reduce_fusion.1
  84.8 1.1 convolution_bitcast_fusion
  86.0 1.4 copy.28
  87.4 56.2 %all_to_all.15 = f32[128,1,8,130]{3,2,1,0:T(8,128)S(1)} all-to-all(f32[128,1,8,130]{3,2,1,0:T(8,128)} %copy.28), channel_id=1, replica_groups=mesh['groups'=2,'seq'=16,'head'=8,'rep'=2] {'seq'}, dimensions={0} | all-to-all | bytes 1064960 | tf_op jit(solution)/shard_map/all_to_all | solution.py:31
  143.6 1.1 fusion.41
  144.7 1.2 copy.29
  145.9 0.1 reshape_reshape.12
  146.0 0.1 reshape_reshape.13
  146.1 1.2 copy.33
  147.3 0.1 reshape_reshape.14
  147.5 0.1 copy.34
  147.6 0.1 copy.30
  147.7 0.2 slice.13
  147.9 0.2 multiply_reduce_fusion
  148.1 0.7 divide_convert_fusion
  (9 shorter events, 0.2 us)
Async XLA Ops:
  0.0 80.6 %copy-start = (bf16[64,1,128,128]{3,2,1,0:T(8,128)(2,1)S(1)}, bf16[64,1,128,128]{3,2,1,0:T(8,128)(2,1)}, u32[]{:S(2)}) copy-start(bf16[64,1,128,128]{3,2,1,0:T(8,128)(2,1)} %param.10) | copy-start | bytes 6291460
  1.6 56.4 %all-to-all-start = ((s32[16,8,128]{2,1,0:T(8,128)}), s32[16,8,128]{2,1,0:T(8,128)S(1)}, u32[]{:S(2)}, u32[]{:S(2)}) async-start(s32[16,8,128]{2,1,0:T(8,128)} %broadcast_in_dim.95), calls=%async_computation | async-start | bytes 131072 | tf_op jit(solution)/shard_map/all_to_all | solution.py:13
  59.4 21.0 %all-to-all-start.1 = ((bf16[16,8,8,128]{3,2,1,0:T(8,128)(2,1)}), bf16[16,8,8,128]{3,2,1,0:T(8,128)(2,1)S(1)}, u32[]{:S(2)}, u32[]{:S(2)}) async-start(bf16[16,8,8,128]{3,2,1,0:T(8,128)(2,1)} %broadcast_in_dim.100), calls=%async_computation.1 | async-start | bytes 524288 | tf_op jit(solution)/shard_map/all_to_all | solution.py:13
where the time goes:
time: 149 us
  blocking collectives  56.2 us (38%)
  starting transfers between devices  47.7 us (32%)
  waiting for transfers between devices  26.9 us (18%)
  local copies, waits for them, and re-layouts  7.79 us (5%)
  other arithmetic  5.3 us (4%)
  matrix products  4.83 us (3%)
    all_to_all x1, blocking collectives, sent_together(): lax.all_to_all(both, axis, split_axis=split_dim, concat_axis=concat_dim,...  56.2 us
    all_to_all x2, starting transfers between devices, sent_to_all(): return lax.all_to_all(copies, axis, split_axis=0, concat_axis=0, tiled=True)  47.7 us
    all_to_all x2, waiting for transfers between devices, sent_to_all(): return lax.all_to_all(copies, axis, split_axis=0, concat_axis=0, tiled=True)  26.9 us
    slice x4, local copies, waits for them, and re-layouts, sent_together(): slab = out[..., at:at + column.shape[along]]  3.78 us
  transfers between devices with their start and end apart: 2, of which 2 were waited for; matrix products, arithmetic and copies ran while one was open for 2% of the time, Pallas kernels for 0%

commit v1 on v0

v1 whole, which is shorter than its diff:
```python
import math

import jax
import jax.numpy as jnp
from jax import lax
from jax.experimental import pallas as pl
from jax.experimental.pallas import tpu as pltpu
from jax.sharding import PartitionSpec as P

masked_score = -1e30
LANES = 128
bf16 = jnp.bfloat16
f32 = jnp.float32
VMEM = pltpu.VMEM


def dot_nt(a, b):
    return lax.dot_general(a, b, (((1,), (1,)), ((), ())), preferred_element_type=f32)


def dot_nn(a, b):
    return lax.dot_general(a, b, (((1,), (0,)), ((), ())), preferred_element_type=f32)


def pieces(x):
    first = x.astype(bf16).astype(f32)
    rest = x - first
    second = rest.astype(bf16).astype(f32)
    third = (rest - second).astype(bf16).astype(f32)
    return first, second, third


def pack_kernel(seq, pool, tokens, q_ref, owner_ref, slot_ref, len_ref, out_ref, q_rows, table):
    rows, heads, width = q_ref.shape
    q_rows[...] = q_ref[...].astype(f32).reshape(rows * heads, width)
    for h in range(heads):
        part = q_rows[pl.ds(h, rows, stride=heads), :]
        many = jnp.concatenate([part] * seq, axis=0).astype(bf16)
        out_ref[:, h * width : (h + 1) * width] = many
    pages = owner_ref.shape[1]
    place = lax.broadcasted_iota(jnp.int32, (1, pages), 1) * tokens
    owner_id = lax.broadcasted_iota(jnp.int32, (seq, pages), 0)
    slot_id = lax.broadcasted_iota(jnp.int32, (LANES, pages), 0)
    for r in range(rows):
        live = jnp.clip(len_ref[r] - place, 0, tokens).astype(f32)
        at = jnp.where(owner_ref[r : r + 1, :] == owner_id, live, 0.0).astype(bf16)
        slot = jnp.where(slot_ref[r : r + 1, :] == slot_id, 1.0, 0.0).astype(bf16)
        table[pl.ds(r, seq, stride=rows), :] = dot_nt(at, slot)
    out_ref[:, heads * width :] = table[...].astype(bf16)


def pages_kernel(pool, heads, in_ref, k_ref, v_ref, out_ref, qs, sc, po):
    width = k_ref.shape[2]
    tokens = k_ref.shape[1]
    reqs = in_ref.shape[0]
    live_of = in_ref[:, heads * width :].astype(f32)
    live_by_page = live_of.T[:pool, :]
    linked_t = live_by_page > 0.0
    live = jnp.max(live_by_page, axis=1, keepdims=True)
    picker = jnp.where(linked_t, 1.0, 0.0).astype(bf16)
    slot_q = dot_nn(picker, in_ref[:, : heads * width])
    for h in range(heads):
        qs[pl.ds(h, pool, stride=heads), :] = slot_q[:, h * width : (h + 1) * width]
    for p in range(pool):
        rows = slice(p * heads, (p + 1) * heads)
        sc[rows, :] = dot_nt(qs[rows, :].astype(bf16), k_ref[p])
    scale = 1.0 / math.sqrt(width)
    mask = lax.broadcasted_iota(jnp.int32, (pool, tokens), 1).astype(f32) < live
    page_max, page_sum = [], []
    for h in range(heads):
        rows = pl.ds(h, pool, stride=heads)
        s = jnp.where(mask, sc[rows, :] * scale, masked_score)
        m = jnp.max(s, axis=1, keepdims=True)
        w = jnp.where(mask, jnp.exp(s - m), 0.0)
        sc[rows, :] = w
        page_max.append(m)
        page_sum.append(jnp.sum(w, axis=1, keepdims=True))
    for p in range(pool):
        rows = slice(p * heads, (p + 1) * heads)
        po[rows, :] = dot_nn(sc[rows, :].astype(bf16), v_ref[p])
    tops, sums, scaled = [], [], []
    for h in range(heads):
        top = jnp.max(jnp.where(linked_t, page_max[h], masked_score), axis=0, keepdims=True)
        page_top = jnp.max(jnp.where(linked_t, top, masked_score), axis=1, keepdims=True)
        rescale = jnp.exp(jnp.minimum(page_max[h] - page_top, 0.0))
        tops.append(top)
        sums.append(
            jnp.sum(jnp.where(linked_t, page_sum[h] * rescale, 0.0), axis=0, keepdims=True)
        )
        scaled.append(po[pl.ds(h, pool, stride=heads), :] * rescale)
    top = jnp.concatenate(tops, axis=0)
    total = jnp.concatenate(sums, axis=0)
    inverse = jnp.where(total > 0.0, 1.0 / jnp.where(total > 0.0, total, 1.0), 0.0)
    m1, m2, m3 = pieces(top)
    s1, s2, s3 = pieces(total)
    filler = jnp.zeros((LANES - 7 * heads, reqs), f32)
    stats = jnp.concatenate([m1, m2, m3, s1, s2, s3, inverse, filler], axis=0).T
    out_ref[:, heads * width :] = stats.astype(bf16)
    linked = jnp.where(live_of[:, :pool] > 0.0, 1.0, 0.0).astype(bf16)
    linked3 = jnp.concatenate([linked] * 3, axis=1)
    for h in range(heads):
        stack = jnp.concatenate(pieces(scaled[h]), axis=0).astype(bf16)
        joined = dot_nn(linked3, stack)
        joined = joined * stats[:, 6 * heads + h : 6 * heads + h + 1]
        out_ref[:, h * width : (h + 1) * width] = joined.astype(bf16)


def merge_kernel(heads, rows, in_ref, out_ref, scratch):
    width = out_ref.shape[1]
    reqs = in_ref.shape[0]
    stats = in_ref[:, heads * width :].astype(f32).T
    part = [stats[k * heads : (k + 1) * heads, :] for k in range(6)]
    top = part[0] + part[1] + part[2]
    total = part[3] + part[4] + part[5]
    overall = top
    step = rows
    while step < reqs:
        overall = jnp.maximum(overall, pltpu.roll(overall, step, 1))
        step *= 2
    share = jnp.exp(top - overall) * total
    whole = share
    step = rows
    while step < reqs:
        whole = whole + pltpu.roll(whole, step, 1)
        step *= 2
    share = share / whole
    filler = jnp.zeros((LANES - heads, reqs), f32)
    share = jnp.concatenate([share, filler], axis=0).T
    for h in range(heads):
        x = in_ref[:, h * width : (h + 1) * width].astype(f32) * share[:, h : h + 1]
        x = jnp.sum(x.reshape(reqs // rows, rows, width), axis=0)
        scratch[pl.ds(h, rows, stride=heads), :] = x
    out_ref[...] = scratch[...].astype(bf16)


def on_device(queries, page_owner, page_slot, lengths, keys, values):
    rows, heads, width = queries.shape
    pool, _, tokens, _ = keys.shape
    seq = lax.axis_size("seq")
    reqs = seq * rows
    row_width = heads * width + LANES
    whole = pl.BlockSpec(memory_space=VMEM)
    packed = pl.pallas_call(
        lambda *refs: pack_kernel(seq, pool, tokens, *refs),
        out_shape=jax.ShapeDtypeStruct((reqs, row_width), bf16),
        in_specs=[whole, whole, whole, pl.BlockSpec(memory_space=pltpu.SMEM)],
        out_specs=whole,
        scratch_shapes=[VMEM((rows * heads, width), f32), VMEM((reqs, LANES), f32)],
        name="pack",
    )(queries, page_owner, page_slot, lengths)
    got = lax.all_to_all(packed, "seq", 0, 0, tiled=True)
    partial = pl.pallas_call(
        lambda *refs: pages_kernel(pool, heads, *refs),
        out_shape=jax.ShapeDtypeStruct((reqs, row_width), bf16),
        in_specs=[whole, whole, whole],
        out_specs=whole,
        scratch_shapes=[VMEM((pool * heads, width), f32)] * 3,
        name="pages",
    )(got, keys.reshape(pool, tokens, width), values.reshape(pool, tokens, width))
    back = lax.all_to_all(partial, "seq", 0, 0, tiled=True)
    out = pl.pallas_call(
        lambda *refs: merge_kernel(heads, rows, *refs),
        out_shape=jax.ShapeDtypeStruct((rows * heads, width), bf16),
        in_specs=[whole],
        out_specs=whole,
        scratch_shapes=[VMEM((rows * heads, width), f32)],
        name="merge",
    )(back)
    return out.reshape(rows, heads, width)


def solution(mesh):
    placed = (
        P(("groups", "seq", "rep"), "head", None),
        P(("groups", "seq", "rep"), None),
        P(("groups", "seq", "rep"), None),
        P(("groups", "seq", "rep")),
        P(("groups", "seq", "rep"), "head", None, None),
        P(("groups", "seq", "rep"), "head", None, None),
    )
    return jax.shard_map(
        on_device,
        mesh=mesh,
        in_specs=placed,
        out_specs=P(("groups", "seq", "rep"), "head", None),
        check_vma=False,
    )
```

time: 149 us -> 98.7 us (0.66)
  starting transfers between devices: 47.7 us -> 0 us
  blocking collectives: 56.2 us -> 88.7 us
  waiting for transfers between devices: 26.9 us -> 0 us
  Pallas kernels: 0 us -> 9.56 us
  local copies, waits for them, and re-layouts: 7.79 us -> 0 us
  other arithmetic: 5.3 us -> 0 us
  matrix products: 4.83 us -> 0 us
    all_to_all x2 -> x0, starting transfers between devices: 47.7 us -> none  [sent_to_all(): return lax.all_to_all(copies, axis, split_axis=0, concat_axis=0, tiled=True)]
    all_to_all x1 -> x2, blocking collectives: 56.2 us -> 88.7 us  [the longest x1 63.1 us: on_device(): got = lax.all_to_all(packed, 'seq', 0, 0, tiled=True)]
    all_to_all x2 -> x0, waiting for transfers between devices: 26.9 us -> none  [sent_to_all(): return lax.all_to_all(copies, axis, split_axis=0, concat_axis=0, tiled=True)]
    pallas_call x0 -> x3, Pallas kernels: none -> 9.56 us  [the longest x1 5.27 us: on_device(): pl.pallas_call(lambda *refs: pages_kernel(pool, heads, *refs), out_shape=...]
    dot_general x4 -> x0, matrix products: 4.83 us -> none  [the longest x1 2.29 us: on_device(): jnp.einsum('pkgt,pktd->pkgd', weights.astype(jnp.bfloat16), values, prefe...]
    slice x4 -> x0, local copies, waits for them, and re-layouts: 3.78 us -> none  [sent_together(): slab = out[..., at:at + column.shape[along]]]
    broadcast_in_dim x2 -> x0, local copies, waits for them, and re-layouts: 2.09 us -> none  [sent_to_all(): copies = jnp.broadcast_to(x, (lax.axis_size(axis), *x.shape))]
    reduce_sum x5 -> x0, other arithmetic: 1.97 us -> none  [the longest x1 1.27 us: on_device(): jnp.sum(jnp.where(matches, live_count[None, :, :], 0), axis=(1, 2))]
  transfers between devices with their start and end apart: 2 -> 0, of which waited for: 2 -> 0; matrix products, arithmetic and copies ran while one was open for 2% -> 0% of each run, Pallas kernels for 0% -> 0%
where the time goes in v1:
time: 98.7 us; the launch traced here: 98.3 us
  blocking collectives  88.7 us (90%)
  Pallas kernels  9.56 us (10%)
    all_to_all x1, blocking collectives, on_device(): got = lax.all_to_all(packed, 'seq', 0, 0, tiled=True)  63.1 us
    all_to_all x1, blocking collectives, on_device(): back = lax.all_to_all(partial, 'seq', 0, 0, tiled=True)  25.6 us
    pallas_call x1, Pallas kernels, on_device(): pl.pallas_call(lambda *refs: pages_kernel(pool, heads, *refs), out_shape=...  5.27 us
    pallas_call x1, Pallas kernels, on_device(): pl.pallas_call(lambda *refs: merge_kernel(heads, rows, *refs), out_shape=...  2.52 us

profile of v1, /device:TPU:80, one launch (start us, length us, event | category | flops | bytes accessed | tf_op | source)
XLA Modules:
  0.0 98.3 jit_solution(2195282820653879346)
XLA Ops:
  0.0 1.8 %pack.1 = bf16[128,1152]{1,0:T(8,128)(2,1)} custom-call(bf16[8,8,128]{2,1,0:T(8,128)(2,1)} %refs_0_.1, s32[8,128]{1,0:T(8,128)} %refs_1_.1, s32[8,128]{1,0:T(8,128)} %refs_2_.1, s32[8]{0:T(128)} %refs_3_.1), custom_call_target="tpu_custom_call" | custom-call | tf_op jit(solution)/shard_map/pack/pallas_call | solution.py:143
  1.8 63.1 %all_to_all.22 = bf16[16,8,1152]{2,1,0:T(8,128)(2,1)} all-to-all(bf16[16,8,1152]{2,1,0:T(8,128)(2,1)} %bitcast.12), channel_id=1, replica_groups=mesh['groups'=2,'seq'=16,'head'=8,'rep'=2] {'seq'}, dimensions={0} | all-to-all | bytes 589824 | tf_op jit(solution)/shard_map/all_to_all | solution.py:151
  64.9 5.3 %pages.1 = bf16[128,1152]{1,0:T(8,128)(2,1)} custom-call(bf16[128,1152]{1,0:T(8,128)(2,1)} %bitcast.9, bf16[64,128,128]{2,1,0:T(8,128)(2,1)} %bitcast.7, bf16[64,128,128]{2,1,0:T(8,128)(2,1)} %bitcast.8), custom_call_target="tpu_custom_call" | custom-call | tf_op jit(solution)/shard_map/pages/pallas_call | solution.py:152
  70.1 25.6 %all_to_all.23 = bf16[16,8,1152]{2,1,0:T(8,128)(2,1)} all-to-all(bf16[16,8,1152]{2,1,0:T(8,128)(2,1)} %bitcast.10), channel_id=1, replica_groups=mesh['groups'=2,'seq'=16,'head'=8,'rep'=2] {'seq'}, dimensions={0} | all-to-all | bytes 589824 | tf_op jit(solution)/shard_map/all_to_all | solution.py:160
  95.8 2.5 %merge.1 = bf16[64,128]{1,0:T(8,128)(2,1)} custom-call(bf16[128,1152]{1,0:T(8,128)(2,1)} %bitcast.11), custom_call_target="tpu_custom_call" | custom-call | tf_op jit(solution)/shard_map/merge/pallas_call | solution.py:161

commit v2 on v1

--- a/solution.py
+++ b/solution.py
@@ -30,13 +30,15 @@
     return first, second, third
 
 
-def pack_kernel(seq, pool, tokens, q_ref, owner_ref, slot_ref, len_ref, out_ref, q_rows, table):
+def pack_kernel(seq, tokens, q_hbm, owner_hbm, slot_hbm, len_hbm, out_ref, *scratch):
+    q_ref, owner_ref, slot_ref, len_ref, sems, q_rows, table = scratch
+    pairs = (len_hbm, len_ref), (owner_hbm, owner_ref), (slot_hbm, slot_ref), (q_hbm, q_ref)
+    loads = [pltpu.make_async_copy(a, b, sems.at[i]) for i, (a, b) in enumerate(pairs)]
+    for load in loads:
+        load.start()
     rows, heads, width = q_ref.shape
-    q_rows[...] = q_ref[...].astype(f32).reshape(rows * heads, width)
-    for h in range(heads):
-        part = q_rows[pl.ds(h, rows, stride=heads), :]
-        many = jnp.concatenate([part] * seq, axis=0).astype(bf16)
-        out_ref[:, h * width : (h + 1) * width] = many
+    for load in loads[:3]:
+        load.wait()
     pages = owner_ref.shape[1]
     place = lax.broadcasted_iota(jnp.int32, (1, pages), 1) * tokens
     owner_id = lax.broadcasted_iota(jnp.int32, (seq, pages), 0)
@@ -47,6 +49,12 @@
         slot = jnp.where(slot_ref[r : r + 1, :] == slot_id, 1.0, 0.0).astype(bf16)
         table[pl.ds(r, seq, stride=rows), :] = dot_nt(at, slot)
     out_ref[:, heads * width :] = table[...].astype(bf16)
+    loads[3].wait()
+    q_rows[...] = q_ref[...].astype(f32).reshape(rows * heads, width)
+    for h in range(heads):
+        part = q_rows[pl.ds(h, rows, stride=heads), :]
+        many = jnp.concatenate([part] * seq, axis=0).astype(bf16)
+        out_ref[:, h * width : (h + 1) * width] = many
 
 
 def pages_kernel(pool, heads, in_ref, k_ref, v_ref, out_ref, qs, sc, po):
@@ -140,14 +148,26 @@
     reqs = seq * rows
     row_width = heads * width + LANES
     whole = pl.BlockSpec(memory_space=VMEM)
+    hbm = pl.BlockSpec(memory_space=pltpu.HBM)
+    small = (queries, page_owner, page_slot, lengths)
     packed = pl.pallas_call(
-        lambda *refs: pack_kernel(seq, pool, tokens, *refs),
+        lambda *refs: pack_kernel(seq, tokens, *refs),
         out_shape=jax.ShapeDtypeStruct((reqs, row_width), bf16),
-        in_specs=[whole, whole, whole, pl.BlockSpec(memory_space=pltpu.SMEM)],
+        in_specs=[hbm] * 4,
         out_specs=whole,
-        scratch_shapes=[VMEM((rows * heads, width), f32), VMEM((reqs, LANES), f32)],
+        scratch_shapes=[
+            VMEM(queries.shape, bf16),
+            VMEM(page_owner.shape, jnp.int32),
+            VMEM(page_slot.shape, jnp.int32),
+            pltpu.SMEM(lengths.shape, jnp.int32),
+            pltpu.SemaphoreType.DMA((4,)),
+            VMEM((rows * heads, width), f32),
+            VMEM((reqs, LANES), f32),
+        ],
+        cost_estimate=pl.CostEstimate(flops=1 << 33, bytes_accessed=1 << 19, transcendentals=0),
+        compiler_params=pltpu.CompilerParams(vmem_limit_bytes=4 << 20),
         name="pack",
-    )(queries, page_owner, page_slot, lengths)
+    )(*[pltpu.with_memory_space_constraint(a, pltpu.HBM) for a in small])
     got = lax.all_to_all(packed, "seq", 0, 0, tiled=True)
     partial = pl.pallas_call(
         lambda *refs: pages_kernel(pool, heads, *refs),
@@ -155,6 +175,7 @@
         in_specs=[whole, whole, whole],
         out_specs=whole,
         scratch_shapes=[VMEM((pool * heads, width), f32)] * 3,
+        compiler_params=pltpu.CompilerParams(vmem_limit_bytes=12 << 20),
         name="pages",
     )(got, keys.reshape(pool, tokens, width), values.reshape(pool, tokens, width))
     back = lax.all_to_all(partial, "seq", 0, 0, tiled=True)
@@ -164,6 +185,7 @@
         in_specs=[whole],
         out_specs=whole,
         scratch_shapes=[VMEM((rows * heads, width), f32)],
+        compiler_params=pltpu.CompilerParams(vmem_limit_bytes=4 << 20),
         name="merge",
     )(back)
     return out.reshape(rows, heads, width)

time: 98.7 us -> 93.5 us (0.947)
  Pallas kernels: 9.56 us -> 5.01 us
    pallas_call x1, Pallas kernels: 5.27 us -> 2.25 us  [on_device(): pl.pallas_call(lambda *refs: pages_kernel(pool, heads, *refs), out_shape=...]
where the time goes in v2:
time: 93.5 us; the launch traced here: 93.3 us
  blocking collectives  88.3 us (94%)
  Pallas kernels  5.01 us (5%)
    all_to_all x1, blocking collectives, on_device(): got = lax.all_to_all(packed, 'seq', 0, 0, tiled=True)  62.9 us
    all_to_all x1, blocking collectives, on_device(): back = lax.all_to_all(partial, 'seq', 0, 0, tiled=True)  25.3 us
    pallas_call x1, Pallas kernels, on_device(): pl.pallas_call(lambda *refs: pages_kernel(pool, heads, *refs), out_shape=...  2.25 us

profile of v2, /device:TPU:80, one launch (start us, length us, event | category | flops | bytes accessed | tf_op | source)
XLA Modules:
  0.0 93.3 jit_solution(13484016668601707689)
XLA Ops:
  0.0 0.0 copy-start.1
  0.0 0.0 copy-start
  0.0 1.2 %pack.1 = bf16[128,1152]{1,0:T(8,128)(2,1)S(1)} custom-call(bf16[8,8,128]{2,1,0:T(8,128)(2,1)} %refs_0_.1, s32[8,128]{1,0:T(8,128)} %refs_1_.1, s32[8,128]{1,0:T(8,128)} %refs_2_.1, s32[8]{0:T(128)} %refs_3_.1), custom_call_target="tpu_custom_call" | custom-call | flops 8589934592 | bytes 524288 | tf_op jit(solution)/shard_map/pack/pallas_call | solution.py:153
  1.2 62.9 %all_to_all.22 = bf16[16,8,1152]{2,1,0:T(8,128)(2,1)S(1)} all-to-all(bf16[16,8,1152]{2,1,0:T(8,128)(2,1)S(1)} %bitcast.12), channel_id=1, replica_groups=mesh['groups'=2,'seq'=16,'head'=8,'rep'=2] {'seq'}, dimensions={0} | all-to-all | bytes 589824 | tf_op jit(solution)/shard_map/all_to_all | solution.py:171
  64.1 0.0 copy-done.1
  64.1 0.0 copy-done
  64.1 2.3 %pages.1 = bf16[128,1152]{1,0:T(8,128)(2,1)S(1)} custom-call(bf16[128,1152]{1,0:T(8,128)(2,1)S(1)} %bitcast.9, bf16[64,128,128]{2,1,0:T(8,128)(2,1)S(1)} %bitcast.7, bf16[64,128,128]{2,1,0:T(8,128)(2,1)S(1)} %bitcast.8), custom_call_target="tpu_custom_call" | custom-call | tf_op jit(solution)/shard_map/pages/pallas_call | solution.py:172
  66.4 25.3 %all_to_all.23 = bf16[16,8,1152]{2,1,0:T(8,128)(2,1)S(1)} all-to-all(bf16[16,8,1152]{2,1,0:T(8,128)(2,1)S(1)} %bitcast.10), channel_id=1, replica_groups=mesh['groups'=2,'seq'=16,'head'=8,'rep'=2] {'seq'}, dimensions={0} | all-to-all | bytes 589824 | tf_op jit(solution)/shard_map/all_to_all | solution.py:181
  91.7 1.6 %merge.1 = bf16[64,128]{1,0:T(8,128)(2,1)} custom-call(bf16[128,1152]{1,0:T(8,128)(2,1)S(1)} %bitcast.11), custom_call_target="tpu_custom_call" | custom-call | tf_op jit(solution)/shard_map/merge/pallas_call | solution.py:182
Async XLA Ops:
  0.0 64.1 %copy-start.1 = (bf16[64,1,128,128]{3,2,1,0:T(8,128)(2,1)S(1)}, bf16[64,1,128,128]{3,2,1,0:T(8,128)(2,1)}, u32[]{:S(2)}) copy-start(bf16[64,1,128,128]{3,2,1,0:T(8,128)(2,1)} %param.11) | copy-start | bytes 6291460
  0.0 64.1 %copy-start = (bf16[64,1,128,128]{3,2,1,0:T(8,128)(2,1)S(1)}, bf16[64,1,128,128]{3,2,1,0:T(8,128)(2,1)}, u32[]{:S(2)}) copy-start(bf16[64,1,128,128]{3,2,1,0:T(8,128)(2,1)} %param.10) | copy-start | bytes 6291460

commit v3 on v2

--- a/solution.py
+++ b/solution.py
@@ -9,6 +9,7 @@
 
 masked_score = -1e30
 LANES = 128
+STAGGER_NS = 6000
 bf16 = jnp.bfloat16
 f32 = jnp.float32
 VMEM = pltpu.VMEM
@@ -49,6 +50,11 @@
         slot = jnp.where(slot_ref[r : r + 1, :] == slot_id, 1.0, 0.0).astype(bf16)
         table[pl.ds(r, seq, stride=rows), :] = dot_nt(at, slot)
     out_ref[:, heads * width :] = table[...].astype(bf16)
+
+    @pl.when(lax.axis_index("rep") == 0)
+    def _():
+        pl.delay(STAGGER_NS)
+
     loads[3].wait()
     q_rows[...] = q_ref[...].astype(f32).reshape(rows * heads, width)
     for h in range(heads):
@@ -116,24 +122,18 @@
 def merge_kernel(heads, rows, in_ref, out_ref, scratch):
     width = out_ref.shape[1]
     reqs = in_ref.shape[0]
-    stats = in_ref[:, heads * width :].astype(f32).T
-    part = [stats[k * heads : (k + 1) * heads, :] for k in range(6)]
-    top = part[0] + part[1] + part[2]
-    total = part[3] + part[4] + part[5]
-    overall = top
-    step = rows
-    while step < reqs:
-        overall = jnp.maximum(overall, pltpu.roll(overall, step, 1))
-        step *= 2
-    share = jnp.exp(top - overall) * total
-    whole = share
-    step = rows
-    while step < reqs:
-        whole = whole + pltpu.roll(whole, step, 1)
-        step *= 2
-    share = share / whole
-    filler = jnp.zeros((LANES - heads, reqs), f32)
-    share = jnp.concatenate([share, filler], axis=0).T
+    stats = in_ref[:, heads * width :].astype(f32)
+
+    def lanes_from(x, at):
+        return pltpu.roll(x, LANES - at, 1)
+
+    joined = stats + lanes_from(stats, heads) + lanes_from(stats, 2 * heads)
+    by_source = (reqs // rows, rows, LANES)
+    top = joined.reshape(by_source)
+    total = lanes_from(joined, 3 * heads).reshape(by_source)
+    share = jnp.exp(top - jnp.max(top, axis=0, keepdims=True)) * total
+    share = share * (1.0 / jnp.sum(share, axis=0, keepdims=True))
+    share = share.reshape(reqs, LANES)
     for h in range(heads):
         x = in_ref[:, h * width : (h + 1) * width].astype(f32) * share[:, h : h + 1]
         x = jnp.sum(x.reshape(reqs // rows, rows, width), axis=0)

time: 93.5 us -> 88.7 us (0.949)
  blocking collectives: 88.3 us -> 78 us
  Pallas kernels: 5.01 us -> 10.5 us
    pallas_call x1, Pallas kernels: 1.2 us -> 7.2 us  [on_device(): pl.pallas_call(lambda *refs: pack_kernel(seq, tokens, *refs), out_shape=j...]
    all_to_all x1, blocking collectives: 62.9 us -> 57.5 us  [on_device(): got = lax.all_to_all(packed, 'seq', 0, 0, tiled=True)]
    all_to_all x1, blocking collectives: 25.3 us -> 20.6 us  [on_device(): back = lax.all_to_all(partial, 'seq', 0, 0, tiled=True)]
where the time goes in v3:
time: 88.7 us; the launch traced here: 88.5 us
  blocking collectives  78 us (88%)
  Pallas kernels  10.5 us (12%)
    all_to_all x1, blocking collectives, on_device(): got = lax.all_to_all(packed, 'seq', 0, 0, tiled=True)  57.5 us
    all_to_all x1, blocking collectives, on_device(): back = lax.all_to_all(partial, 'seq', 0, 0, tiled=True)  20.6 us
    pallas_call x1, Pallas kernels, on_device(): pl.pallas_call(lambda *refs: pack_kernel(seq, tokens, *refs), out_shape=j...  7.2 us
    pallas_call x1, Pallas kernels, on_device(): pl.pallas_call(lambda *refs: pages_kernel(pool, heads, *refs), out_shape=...  2.25 us

profile of v3, /device:TPU:80, one launch (start us, length us, event | category | flops | bytes accessed | tf_op | source)
XLA Modules:
  0.0 88.5 jit_solution(4155337536141438527)
XLA Ops:
  0.0 0.0 copy-start.1
  0.0 0.0 copy-start
  0.0 7.2 %pack.1 = bf16[128,1152]{1,0:T(8,128)(2,1)S(1)} custom-call(bf16[8,8,128]{2,1,0:T(8,128)(2,1)} %refs_0_.1, s32[8,128]{1,0:T(8,128)} %refs_1_.1, s32[8,128]{1,0:T(8,128)} %refs_2_.1, s32[8]{0:T(128)} %refs_3_.1), custom_call_target="tpu_custom_call" | custom-call | flops 8589934592 | bytes 524288 | tf_op jit(solution)/shard_map/pack/pallas_call | solution.py:153
  7.2 57.5 %all_to_all.22 = bf16[16,8,1152]{2,1,0:T(8,128)(2,1)S(1)} all-to-all(bf16[16,8,1152]{2,1,0:T(8,128)(2,1)S(1)} %bitcast.12), channel_id=1, replica_groups=mesh['groups'=2,'seq'=16,'head'=8,'rep'=2] {'seq'}, dimensions={0} | all-to-all | bytes 589824 | tf_op jit(solution)/shard_map/all_to_all | solution.py:171
  64.7 0.0 copy-done.1
  64.7 0.0 copy-done
  64.7 2.2 %pages.1 = bf16[128,1152]{1,0:T(8,128)(2,1)S(1)} custom-call(bf16[128,1152]{1,0:T(8,128)(2,1)S(1)} %bitcast.9, bf16[64,128,128]{2,1,0:T(8,128)(2,1)S(1)} %bitcast.7, bf16[64,128,128]{2,1,0:T(8,128)(2,1)S(1)} %bitcast.8), custom_call_target="tpu_custom_call" | custom-call | tf_op jit(solution)/shard_map/pages/pallas_call | solution.py:172
  66.9 20.6 %all_to_all.23 = bf16[16,8,1152]{2,1,0:T(8,128)(2,1)S(1)} all-to-all(bf16[16,8,1152]{2,1,0:T(8,128)(2,1)S(1)} %bitcast.10), channel_id=1, replica_groups=mesh['groups'=2,'seq'=16,'head'=8,'rep'=2] {'seq'}, dimensions={0} | all-to-all | bytes 589824 | tf_op jit(solution)/shard_map/all_to_all | solution.py:181
  87.5 1.0 %merge.1 = bf16[64,128]{1,0:T(8,128)(2,1)} custom-call(bf16[128,1152]{1,0:T(8,128)(2,1)S(1)} %bitcast.11), custom_call_target="tpu_custom_call" | custom-call | tf_op jit(solution)/shard_map/merge/pallas_call | solution.py:182
Async XLA Ops:
  0.0 64.7 %copy-start.1 = (bf16[64,1,128,128]{3,2,1,0:T(8,128)(2,1)S(1)}, bf16[64,1,128,128]{3,2,1,0:T(8,128)(2,1)}, u32[]{:S(2)}) copy-start(bf16[64,1,128,128]{3,2,1,0:T(8,128)(2,1)} %param.11) | copy-start | bytes 6291460
  0.0 64.7 %copy-start = (bf16[64,1,128,128]{3,2,1,0:T(8,128)(2,1)S(1)}, bf16[64,1,128,128]{3,2,1,0:T(8,128)(2,1)}, u32[]{:S(2)}) copy-start(bf16[64,1,128,128]{3,2,1,0:T(8,128)(2,1)} %param.10) | copy-start | bytes 6291460

commit v4 on v3

--- a/solution.py
+++ b/solution.py
@@ -9,7 +9,8 @@
 
 masked_score = -1e30
 LANES = 128
-STAGGER_NS = 6000
+PIECES = 3
+STAGGER_NS = 5000
 bf16 = jnp.bfloat16
 f32 = jnp.float32
 VMEM = pltpu.VMEM
@@ -29,6 +30,30 @@
     second = rest.astype(bf16).astype(f32)
     third = (rest - second).astype(bf16).astype(f32)
     return first, second, third
+
+
+def chunk_rows(d, h, rows, heads):
+    at = d * (rows * heads + rows // 2) + h * rows
+    return slice(at, at + rows)
+
+
+def fold(ref, x, rows, heads):
+    half = rows // 2
+    for d in range(x.shape[0] // rows):
+        piece = x[d * rows : (d + 1) * rows, :]
+        other = pltpu.roll(pltpu.roll(piece, half, 0), LANES // 2, 1)
+        at = chunk_rows(d, heads, rows, heads).start
+        ref[at : at + half, :] = (piece + other)[:half, :].astype(bf16)
+
+
+def unfold(ref, rows, heads):
+    half = rows // 2
+    out = []
+    for d in range(ref.shape[0] // (rows * heads + half)):
+        at = chunk_rows(d, heads, rows, heads).start
+        piece = ref[at : at + half, :].astype(f32)
+        out += [piece, pltpu.roll(piece, LANES // 2, 1)]
+    return jnp.concatenate(out, axis=0)
 
 
 def pack_kernel(seq, tokens, q_hbm, owner_hbm, slot_hbm, len_hbm, out_ref, *scratch):
@@ -49,7 +74,7 @@
         at = jnp.where(owner_ref[r : r + 1, :] == owner_id, live, 0.0).astype(bf16)
         slot = jnp.where(slot_ref[r : r + 1, :] == slot_id, 1.0, 0.0).astype(bf16)
         table[pl.ds(r, seq, stride=rows), :] = dot_nt(at, slot)
-    out_ref[:, heads * width :] = table[...].astype(bf16)
+    fold(out_ref, table[...], rows, heads)
 
     @pl.when(lax.axis_index("rep") == 0)
     def _():
@@ -59,39 +84,57 @@
     q_rows[...] = q_ref[...].astype(f32).reshape(rows * heads, width)
     for h in range(heads):
         part = q_rows[pl.ds(h, rows, stride=heads), :]
-        many = jnp.concatenate([part] * seq, axis=0).astype(bf16)
-        out_ref[:, h * width : (h + 1) * width] = many
-
-
-def pages_kernel(pool, heads, in_ref, k_ref, v_ref, out_ref, qs, sc, po):
+        part = part.astype(bf16)
+        for d in range(seq):
+            out_ref[chunk_rows(d, h, rows, heads), :] = part
+
+
+def side_by_side(ref, p, heads):
+    first = ref[p * heads : (p + 1) * heads, :]
+    second = ref[(p + 1) * heads : (p + 2) * heads, :]
+    none = jnp.zeros_like(first)
+    left = jnp.concatenate([first, none], axis=0)
+    right = jnp.concatenate([none, second], axis=0)
+    return jnp.concatenate([left, right], axis=1).astype(bf16)
+
+
+def pages_kernel(pool, heads, rows, in_ref, k_ref, v_ref, out_ref, qs, sc, po):
     width = k_ref.shape[2]
     tokens = k_ref.shape[1]
-    reqs = in_ref.shape[0]
-    live_of = in_ref[:, heads * width :].astype(f32)
+    live_of = unfold(in_ref, rows, heads)
+    reqs = live_of.shape[0]
     live_by_page = live_of.T[:pool, :]
     linked_t = live_by_page > 0.0
     live = jnp.max(live_by_page, axis=1, keepdims=True)
     picker = jnp.where(linked_t, 1.0, 0.0).astype(bf16)
-    slot_q = dot_nn(picker, in_ref[:, : heads * width])
-    for h in range(heads):
-        qs[pl.ds(h, pool, stride=heads), :] = slot_q[:, h * width : (h + 1) * width]
-    for p in range(pool):
-        rows = slice(p * heads, (p + 1) * heads)
-        sc[rows, :] = dot_nt(qs[rows, :].astype(bf16), k_ref[p])
+    seq = reqs // rows
+    for h in range(0, heads, 2):
+        asked = [
+            jnp.concatenate(
+                [in_ref[chunk_rows(d, h + i, rows, heads), :].astype(f32) for d in range(seq)], axis=0
+            )
+            for i in range(2)
+        ]
+        slot_q = dot_nn(picker, jnp.concatenate(asked, axis=1).astype(bf16))
+        for i in range(2):
+            qs[pl.ds(h + i, pool, stride=heads), :] = slot_q[:, i * width : (i + 1) * width]
+    for p in range(0, pool, 2):
+        both = jnp.concatenate([k_ref[p], k_ref[p + 1]], axis=1)
+        sc[p * heads : (p + 2) * heads, :] = dot_nt(side_by_side(qs, p, heads), both)
     scale = 1.0 / math.sqrt(width)
     mask = lax.broadcasted_iota(jnp.int32, (pool, tokens), 1).astype(f32) < live
     page_max, page_sum = [], []
     for h in range(heads):
-        rows = pl.ds(h, pool, stride=heads)
-        s = jnp.where(mask, sc[rows, :] * scale, masked_score)
+        of_head = pl.ds(h, pool, stride=heads)
+        s = jnp.where(mask, sc[of_head, :] * scale, masked_score)
         m = jnp.max(s, axis=1, keepdims=True)
         w = jnp.where(mask, jnp.exp(s - m), 0.0)
-        sc[rows, :] = w
+        sc[of_head, :] = w
         page_max.append(m)
         page_sum.append(jnp.sum(w, axis=1, keepdims=True))
-    for p in range(pool):
-        rows = slice(p * heads, (p + 1) * heads)
-        po[rows, :] = dot_nn(sc[rows, :].astype(bf16), v_ref[p])
+    for p in range(0, pool, 2):
+        both = v_ref[p : p + 2].reshape(2 * tokens, width)
+        po[p * heads : (p + 2) * heads, :] = dot_nn(side_by_side(sc, p, heads), both)
     tops, sums, scaled = [], [], []
     for h in range(heads):
         top = jnp.max(jnp.where(linked_t, page_max[h], masked_score), axis=0, keepdims=True)
@@ -109,20 +152,23 @@
     s1, s2, s3 = pieces(total)
     filler = jnp.zeros((LANES - 7 * heads, reqs), f32)
     stats = jnp.concatenate([m1, m2, m3, s1, s2, s3, inverse, filler], axis=0).T
-    out_ref[:, heads * width :] = stats.astype(bf16)
+    fold(out_ref, stats, rows, heads)
     linked = jnp.where(live_of[:, :pool] > 0.0, 1.0, 0.0).astype(bf16)
-    linked3 = jnp.concatenate([linked] * 3, axis=1)
-    for h in range(heads):
-        stack = jnp.concatenate(pieces(scaled[h]), axis=0).astype(bf16)
-        joined = dot_nn(linked3, stack)
-        joined = joined * stats[:, 6 * heads + h : 6 * heads + h + 1]
-        out_ref[:, h * width : (h + 1) * width] = joined.astype(bf16)
+    linked = jnp.concatenate([linked] * PIECES, axis=1)
+    for h in range(0, heads, 2):
+        stack = [jnp.concatenate(pieces(x)[:PIECES], axis=0) for x in scaled[h : h + 2]]
+        both = dot_nn(linked, jnp.concatenate(stack, axis=1).astype(bf16))
+        for i in range(2):
+            joined = both[:, i * width : (i + 1) * width]
+            joined = joined * stats[:, 6 * heads + h + i : 6 * heads + h + i + 1]
+            for d in range(seq):
+                piece = joined[d * rows : (d + 1) * rows, :].astype(bf16)
+                out_ref[chunk_rows(d, h + i, rows, heads), :] = piece
 
 
 def merge_kernel(heads, rows, in_ref, out_ref, scratch):
-    width = out_ref.shape[1]
-    reqs = in_ref.shape[0]
-    stats = in_ref[:, heads * width :].astype(f32)
+    stats = unfold(in_ref, rows, heads)
+    reqs = stats.shape[0]
 
     def lanes_from(x, at):
         return pltpu.roll(x, LANES - at, 1)
@@ -135,9 +181,12 @@
     share = share * (1.0 / jnp.sum(share, axis=0, keepdims=True))
     share = share.reshape(reqs, LANES)
     for h in range(heads):
-        x = in_ref[:, h * width : (h + 1) * width].astype(f32) * share[:, h : h + 1]
-        x = jnp.sum(x.reshape(reqs // rows, rows, width), axis=0)
-        scratch[pl.ds(h, rows, stride=heads), :] = x
+        total = None
+        for d in range(reqs // rows):
+            x = in_ref[chunk_rows(d, h, rows, heads), :].astype(f32)
+            x = x * share[d * rows : (d + 1) * rows, h : h + 1]
+            total = x if total is None else total + x
+        scratch[pl.ds(h, rows, stride=heads), :] = total
     out_ref[...] = scratch[...].astype(bf16)
 
 
@@ -146,13 +195,13 @@
     pool, _, tokens, _ = keys.shape
     seq = lax.axis_size("seq")
     reqs = seq * rows
-    row_width = heads * width + LANES
+    chunk = rows * heads + rows // 2
     whole = pl.BlockSpec(memory_space=VMEM)
     hbm = pl.BlockSpec(memory_space=pltpu.HBM)
     small = (queries, page_owner, page_slot, lengths)
     packed = pl.pallas_call(
         lambda *refs: pack_kernel(seq, tokens, *refs),
-        out_shape=jax.ShapeDtypeStruct((reqs, row_width), bf16),
+        out_shape=jax.ShapeDtypeStruct((seq * chunk, width), bf16),
         in_specs=[hbm] * 4,
         out_specs=whole,
         scratch_shapes=[
@@ -168,17 +217,22 @@
         compiler_params=pltpu.CompilerParams(vmem_limit_bytes=4 << 20),
         name="pack",
     )(*[pltpu.with_memory_space_constraint(a, pltpu.HBM) for a in small])
-    got = lax.all_to_all(packed, "seq", 0, 0, tiled=True)
+
+    def exchange(x):
+        x = x.reshape(seq, 2 * chunk // rows, rows // 2, width)
+        return lax.all_to_all(x, "seq", 0, 0, tiled=True).reshape(seq * chunk, width)
+
+    got = exchange(packed)
     partial = pl.pallas_call(
-        lambda *refs: pages_kernel(pool, heads, *refs),
-        out_shape=jax.ShapeDtypeStruct((reqs, row_width), bf16),
+        lambda *refs: pages_kernel(pool, heads, rows, *refs),
+        out_shape=jax.ShapeDtypeStruct((seq * chunk, width), bf16),
         in_specs=[whole, whole, whole],
         out_specs=whole,
         scratch_shapes=[VMEM((pool * heads, width), f32)] * 3,
         compiler_params=pltpu.CompilerParams(vmem_limit_bytes=12 << 20),
         name="pages",
     )(got, keys.reshape(pool, tokens, width), values.reshape(pool, tokens, width))
-    back = lax.all_to_all(partial, "seq", 0, 0, tiled=True)
+    back = exchange(partial)
     out = pl.pallas_call(
         lambda *refs: merge_kernel(heads, rows, *refs),
         out_shape=jax.ShapeDtypeStruct((rows * heads, width), bf16),

time: 88.7 us -> 86.7 us (0.977)
  Pallas kernels: 10.5 us -> 9.02 us
    pallas_call x1, Pallas kernels: 7.2 us -> 6.29 us  [on_device(): pl.pallas_call(lambda *refs: pack_kernel(seq, tokens, *refs), out_shape=j...]
where the time goes in v4:
time: 86.7 us; the launch traced here: 86.5 us
  blocking collectives  77.5 us (89%)
  Pallas kernels  9.02 us (10%)
    all_to_all x2, blocking collectives, exchange(): lax.all_to_all(x, 'seq', 0, 0, tiled=True).reshape(seq * chunk, width)  77.5 us
    pallas_call x1, Pallas kernels, on_device(): pl.pallas_call(lambda *refs: pack_kernel(seq, tokens, *refs), out_shape=j...  6.29 us

profile of v4, /device:TPU:80, one launch (start us, length us, event | category | flops | bytes accessed | tf_op | source)
XLA Modules:
  0.0 86.5 jit_solution(7914699117450979841)
XLA Ops:
  0.0 0.0 copy-start.1
  0.0 0.0 copy-start
  0.0 6.3 %pack.1 = bf16[1088,128]{1,0:T(8,128)(2,1)S(1)} custom-call(bf16[8,8,128]{2,1,0:T(8,128)(2,1)} %refs_0_.1, s32[8,128]{1,0:T(8,128)} %refs_1_.1, s32[8,128]{1,0:T(8,128)} %refs_2_.1, s32[8]{0:T(128)} %refs_3_.1), custom_call_target="tpu_custom_call" | custom-call | flops 8589934592 | bytes 524288 | tf_op jit(solution)/shard_map/pack/pallas_call | solution.py:202
  6.3 57.9 %all_to_all.10 = bf16[16,17,4,128]{3,2,1,0:T(4,128)(2,1)S(1)} all-to-all(bf16[16,17,4,128]{3,2,1,0:T(4,128)(2,1)S(1)} %bitcast.12), channel_id=1, replica_groups=mesh['groups'=2,'seq'=16,'head'=8,'rep'=2] {'seq'}, dimensions={0} | all-to-all | bytes 557056 | tf_op jit(solution)/shard_map/all_to_all | solution.py:223
  64.2 0.0 copy-done.1
  64.3 0.0 copy-done
  64.3 1.6 %pages.1 = bf16[1088,128]{1,0:T(8,128)(2,1)S(1)} custom-call(bf16[1088,128]{1,0:T(8,128)(2,1)S(1)} %bitcast.9, bf16[64,128,128]{2,1,0:T(8,128)(2,1)S(1)} %bitcast.7, bf16[64,128,128]{2,1,0:T(8,128)(2,1)S(1)} %bitcast.8), custom_call_target="tpu_custom_call" | custom-call | tf_op jit(solution)/shard_map/pages/pallas_call | solution.py:226
  65.9 19.5 %all_to_all.11 = bf16[16,17,4,128]{3,2,1,0:T(4,128)(2,1)S(1)} all-to-all(bf16[16,17,4,128]{3,2,1,0:T(4,128)(2,1)S(1)} %bitcast.10), channel_id=1, replica_groups=mesh['groups'=2,'seq'=16,'head'=8,'rep'=2] {'seq'}, dimensions={0} | all-to-all | bytes 557056 | tf_op jit(solution)/shard_map/all_to_all | solution.py:223
  85.4 1.1 %merge.1 = bf16[64,128]{1,0:T(8,128)(2,1)} custom-call(bf16[1088,128]{1,0:T(8,128)(2,1)S(1)} %bitcast.11), custom_call_target="tpu_custom_call" | custom-call | tf_op jit(solution)/shard_map/merge/pallas_call | solution.py:236
Async XLA Ops:
  0.0 64.3 %copy-start.1 = (bf16[64,1,128,128]{3,2,1,0:T(8,128)(2,1)S(1)}, bf16[64,1,128,128]{3,2,1,0:T(8,128)(2,1)}, u32[]{:S(2)}) copy-start(bf16[64,1,128,128]{3,2,1,0:T(8,128)(2,1)} %param.11) | copy-start | bytes 6291460
  0.0 64.3 %copy-start = (bf16[64,1,128,128]{3,2,1,0:T(8,128)(2,1)S(1)}, bf16[64,1,128,128]{3,2,1,0:T(8,128)(2,1)}, u32[]{:S(2)}) copy-start(bf16[64,1,128,128]{3,2,1,0:T(8,128)(2,1)} %param.10) | copy-start | bytes 6291460

commit v5 on v4

--- a/solution.py
+++ b/solution.py
@@ -9,6 +9,7 @@
 
 masked_score = -1e30
 LANES = 128
+EXTRA = 2
 PIECES = 3
 STAGGER_NS = 5000
 bf16 = jnp.bfloat16
@@ -33,27 +34,22 @@
 
 
 def chunk_rows(d, h, rows, heads):
-    at = d * (rows * heads + rows // 2) + h * rows
-    return slice(at, at + rows)
-
-
-def fold(ref, x, rows, heads):
-    half = rows // 2
-    for d in range(x.shape[0] // rows):
-        piece = x[d * rows : (d + 1) * rows, :]
-        other = pltpu.roll(pltpu.roll(piece, half, 0), LANES // 2, 1)
-        at = chunk_rows(d, heads, rows, heads).start
-        ref[at : at + half, :] = (piece + other)[:half, :].astype(bf16)
-
-
-def unfold(ref, rows, heads):
-    half = rows // 2
-    out = []
-    for d in range(ref.shape[0] // (rows * heads + half)):
-        at = chunk_rows(d, heads, rows, heads).start
-        piece = ref[at : at + half, :].astype(f32)
-        out += [piece, pltpu.roll(piece, LANES // 2, 1)]
-    return jnp.concatenate(out, axis=0)
+    at = d * (rows * heads + EXTRA) + h * rows
+    return slice(at, at + (rows if h < heads else EXTRA))
+
+
+def fold(x, rows):
+    half, shift = rows // 2, LANES // 2
+    while half >= EXTRA:
+        x = x + pltpu.roll(pltpu.roll(x, rows - half, 0), shift, 1)
+        half, shift = half // 2, shift // 2
+    return x[:EXTRA, :]
+
+
+def unfold(x, rows):
+    step = LANES * EXTRA // rows
+    parts = [x] + [pltpu.roll(x, LANES - i * step, 1) for i in range(1, rows // EXTRA)]
+    return jnp.concatenate(parts, axis=0)
 
 
 def pack_kernel(seq, tokens, q_hbm, owner_hbm, slot_hbm, len_hbm, out_ref, *scratch):
@@ -69,12 +65,25 @@
     place = lax.broadcasted_iota(jnp.int32, (1, pages), 1) * tokens
     owner_id = lax.broadcasted_iota(jnp.int32, (seq, pages), 0)
     slot_id = lax.broadcasted_iota(jnp.int32, (LANES, pages), 0)
+    half = LANES // 2
+    codes = None
     for r in range(rows):
         live = jnp.clip(len_ref[r] - place, 0, tokens).astype(f32)
-        at = jnp.where(owner_ref[r : r + 1, :] == owner_id, live, 0.0).astype(bf16)
-        slot = jnp.where(slot_ref[r : r + 1, :] == slot_id, 1.0, 0.0).astype(bf16)
-        table[pl.ds(r, seq, stride=rows), :] = dot_nt(at, slot)
-    fold(out_ref, table[...], rows, heads)
+        here = owner_ref[r : r + 1, :] == owner_id
+        slot = slot_ref[r : r + 1, :]
+        number = jnp.where(here, r + 1.0, 0.0).astype(bf16)
+        count = jnp.where(here, live, 0.0).astype(bf16)
+        low = jnp.where(slot == slot_id, 1.0, 0.0).astype(bf16)
+        high = jnp.where(slot + half == slot_id, 1.0, 0.0).astype(bf16)
+        both = dot_nt(
+            jnp.concatenate([number, count], axis=1), jnp.concatenate([low, high], axis=1)
+        )
+        codes = both if codes is None else codes + both
+    table[...] = jnp.zeros_like(table)
+    table[pl.ds(0, seq, stride=EXTRA), :] = codes
+    for d in range(seq):
+        code = table[d * EXTRA : (d + 1) * EXTRA, :].astype(bf16)
+        out_ref[chunk_rows(d, heads, rows, heads), :] = code
 
     @pl.when(lax.axis_index("rep") == 0)
     def _():
@@ -101,13 +110,19 @@
 def pages_kernel(pool, heads, rows, in_ref, k_ref, v_ref, out_ref, qs, sc, po):
     width = k_ref.shape[2]
     tokens = k_ref.shape[1]
-    live_of = unfold(in_ref, rows, heads)
-    reqs = live_of.shape[0]
+    seq = in_ref.shape[0] // (rows * heads + EXTRA)
+    reqs = seq * rows
+    number = lax.broadcasted_iota(jnp.int32, (rows, LANES), 0).astype(f32) + 1.0
+    live_of = []
+    for d in range(seq):
+        code = in_ref[chunk_rows(d, heads, rows, heads), :].astype(f32)
+        code = jnp.broadcast_to(code[:1, :], (rows, LANES))
+        live_of.append(jnp.where(code == number, pltpu.roll(code, LANES // 2, 1), 0.0))
+    live_of = jnp.concatenate(live_of, axis=0)
     live_by_page = live_of.T[:pool, :]
     linked_t = live_by_page > 0.0
     live = jnp.max(live_by_page, axis=1, keepdims=True)
     picker = jnp.where(linked_t, 1.0, 0.0).astype(bf16)
-    seq = reqs // rows
     for h in range(0, heads, 2):
         asked = [
             jnp.concatenate(
@@ -148,11 +163,14 @@
     top = jnp.concatenate(tops, axis=0)
     total = jnp.concatenate(sums, axis=0)
     inverse = jnp.where(total > 0.0, 1.0 / jnp.where(total > 0.0, total, 1.0), 0.0)
-    m1, m2, m3 = pieces(top)
-    s1, s2, s3 = pieces(total)
-    filler = jnp.zeros((LANES - 7 * heads, reqs), f32)
-    stats = jnp.concatenate([m1, m2, m3, s1, s2, s3, inverse, filler], axis=0).T
-    fold(out_ref, stats, rows, heads)
+    high, low, _ = pieces(top)
+    total = total * jnp.exp(jnp.where(total > 0.0, top - (high + low), 0.0))
+    filler = jnp.zeros((LANES - 5 * heads, reqs), f32)
+    stats = jnp.concatenate([high, low, *pieces(total)[:2], inverse, filler], axis=0).T
+    sent = lax.broadcasted_iota(jnp.int32, (rows, LANES), 1) < 4 * heads
+    for d in range(seq):
+        piece = jnp.where(sent, stats[d * rows : (d + 1) * rows, :], 0.0)
+        out_ref[chunk_rows(d, heads, rows, heads), :] = fold(piece, rows).astype(bf16)
     linked = jnp.where(live_of[:, :pool] > 0.0, 1.0, 0.0).astype(bf16)
     linked = jnp.concatenate([linked] * PIECES, axis=1)
     for h in range(0, heads, 2):
@@ -160,29 +178,27 @@
         both = dot_nn(linked, jnp.concatenate(stack, axis=1).astype(bf16))
         for i in range(2):
             joined = both[:, i * width : (i + 1) * width]
-            joined = joined * stats[:, 6 * heads + h + i : 6 * heads + h + i + 1]
+            joined = joined * stats[:, 4 * heads + h + i : 4 * heads + h + i + 1]
             for d in range(seq):
                 piece = joined[d * rows : (d + 1) * rows, :].astype(bf16)
                 out_ref[chunk_rows(d, h + i, rows, heads), :] = piece
 
 
 def merge_kernel(heads, rows, in_ref, out_ref, scratch):
-    stats = unfold(in_ref, rows, heads)
-    reqs = stats.shape[0]
-
-    def lanes_from(x, at):
-        return pltpu.roll(x, LANES - at, 1)
-
-    joined = stats + lanes_from(stats, heads) + lanes_from(stats, 2 * heads)
-    by_source = (reqs // rows, rows, LANES)
-    top = joined.reshape(by_source)
-    total = lanes_from(joined, 3 * heads).reshape(by_source)
+    seq = in_ref.shape[0] // (rows * heads + EXTRA)
+    stats = [
+        unfold(in_ref[chunk_rows(d, heads, rows, heads), :].astype(f32), rows) for d in range(seq)
+    ]
+    stats = jnp.concatenate(stats, axis=0)
+    joined = stats + pltpu.roll(stats, LANES - heads, 1)
+    top = joined.reshape(seq, rows, LANES)
+    total = pltpu.roll(joined, LANES - 2 * heads, 1).reshape(seq, rows, LANES)
     share = jnp.exp(top - jnp.max(top, axis=0, keepdims=True)) * total
     share = share * (1.0 / jnp.sum(share, axis=0, keepdims=True))
-    share = share.reshape(reqs, LANES)
+    share = share.reshape(seq * rows, LANES)
     for h in range(heads):
         total = None
-        for d in range(reqs // rows):
+        for d in range(seq):
             x = in_ref[chunk_rows(d, h, rows, heads), :].astype(f32)
             x = x * share[d * rows : (d + 1) * rows, h : h + 1]
             total = x if total is None else total + x
@@ -195,7 +211,7 @@
     pool, _, tokens, _ = keys.shape
     seq = lax.axis_size("seq")
     reqs = seq * rows
-    chunk = rows * heads + rows // 2
+    chunk = rows * heads + EXTRA
     whole = pl.BlockSpec(memory_space=VMEM)
     hbm = pl.BlockSpec(memory_space=pltpu.HBM)
     small = (queries, page_owner, page_slot, lengths)
@@ -211,7 +227,7 @@
             pltpu.SMEM(lengths.shape, jnp.int32),
             pltpu.SemaphoreType.DMA((4,)),
             VMEM((rows * heads, width), f32),
-            VMEM((reqs, LANES), f32),
+            VMEM((seq * EXTRA, LANES), f32),
         ],
         cost_estimate=pl.CostEstimate(flops=1 << 33, bytes_accessed=1 << 19, transcendentals=0),
         compiler_params=pltpu.CompilerParams(vmem_limit_bytes=4 << 20),
@@ -219,7 +235,7 @@
     )(*[pltpu.with_memory_space_constraint(a, pltpu.HBM) for a in small])
 
     def exchange(x):
-        x = x.reshape(seq, 2 * chunk // rows, rows // 2, width)
+        x = x.reshape(seq, chunk // EXTRA, EXTRA, width)
         return lax.all_to_all(x, "seq", 0, 0, tiled=True).reshape(seq * chunk, width)
 
     got = exchange(packed)

time: 86.7 us -> 86.5 us (level)
  no operation moved by 1% of the time
where the time goes in v5:
time: 86.5 us; the launch traced here: 86.3 us
  blocking collectives  77.2 us (89%)
  Pallas kernels  9.06 us (10%)
    all_to_all x2, blocking collectives, exchange(): lax.all_to_all(x, 'seq', 0, 0, tiled=True).reshape(seq * chunk, width)  77.2 us
    pallas_call x1, Pallas kernels, on_device(): pl.pallas_call(lambda *refs: pack_kernel(seq, tokens, *refs), out_shape=j...  6.23 us
    pallas_call x1, Pallas kernels, on_device(): pl.pallas_call(lambda *refs: pages_kernel(pool, heads, rows, *refs), out_...  1.73 us

profile of v5, /device:TPU:80, one launch (start us, length us, event | category | flops | bytes accessed | tf_op | source)
XLA Modules:
  0.0 86.3 jit_solution(8811443176257785946)
XLA Ops:
  0.0 0.0 copy-start.1
  0.0 0.0 copy-start
  0.0 6.2 %pack.1 = bf16[1056,128]{1,0:T(8,128)(2,1)S(1)} custom-call(bf16[8,8,128]{2,1,0:T(8,128)(2,1)} %refs_0_.1, s32[8,128]{1,0:T(8,128)} %refs_1_.1, s32[8,128]{1,0:T(8,128)} %refs_2_.1, s32[8]{0:T(128)} %refs_3_.1), custom_call_target="tpu_custom_call" | custom-call | flops 8589934592 | bytes 524288 | tf_op jit(solution)/shard_map/pack/pallas_call | solution.py:218
  6.2 57.9 %all_to_all.10 = bf16[16,33,2,128]{3,2,1,0:T(2,128)(2,1)S(1)} all-to-all(bf16[16,33,2,128]{3,2,1,0:T(2,128)(2,1)S(1)} %bitcast.12), channel_id=1, replica_groups=mesh['groups'=2,'seq'=16,'head'=8,'rep'=2] {'seq'}, dimensions={0} | all-to-all | bytes 540672 | tf_op jit(solution)/shard_map/all_to_all | solution.py:239
  64.2 0.0 copy-done.1
  64.2 0.0 copy-done
  64.2 1.7 %pages.1 = bf16[1056,128]{1,0:T(8,128)(2,1)S(1)} custom-call(bf16[1056,128]{1,0:T(8,128)(2,1)S(1)} %bitcast.9, bf16[64,128,128]{2,1,0:T(8,128)(2,1)S(1)} %bitcast.7, bf16[64,128,128]{2,1,0:T(8,128)(2,1)S(1)} %bitcast.8), custom_call_target="tpu_custom_call" | custom-call | tf_op jit(solution)/shard_map/pages/pallas_call | solution.py:242
  65.9 19.3 %all_to_all.11 = bf16[16,33,2,128]{3,2,1,0:T(2,128)(2,1)S(1)} all-to-all(bf16[16,33,2,128]{3,2,1,0:T(2,128)(2,1)S(1)} %bitcast.10), channel_id=1, replica_groups=mesh['groups'=2,'seq'=16,'head'=8,'rep'=2] {'seq'}, dimensions={0} | all-to-all | bytes 540672 | tf_op jit(solution)/shard_map/all_to_all | solution.py:239
  85.2 1.1 %merge.1 = bf16[64,128]{1,0:T(8,128)(2,1)} custom-call(bf16[1056,128]{1,0:T(8,128)(2,1)S(1)} %bitcast.11), custom_call_target="tpu_custom_call" | custom-call | tf_op jit(solution)/shard_map/merge/pallas_call | solution.py:252
Async XLA Ops:
  0.0 64.2 %copy-start.1 = (bf16[64,1,128,128]{3,2,1,0:T(8,128)(2,1)S(1)}, bf16[64,1,128,128]{3,2,1,0:T(8,128)(2,1)}, u32[]{:S(2)}) copy-start(bf16[64,1,128,128]{3,2,1,0:T(8,128)(2,1)} %param.11) | copy-start | bytes 6291460
  0.0 64.2 %copy-start = (bf16[64,1,128,128]{3,2,1,0:T(8,128)(2,1)S(1)}, bf16[64,1,128,128]{3,2,1,0:T(8,128)(2,1)}, u32[]{:S(2)}) copy-start(bf16[64,1,128,128]{3,2,1,0:T(8,128)(2,1)} %param.10) | copy-start | bytes 6291460
